TPU v7x, 768 devices: a whole 4x8x12 slice. The times are simulated.
768 devices in a mesh: shard: 64 (over x, y, core), rep: 12 (over z).
Axes of the slice: x: 4, y: 8, z: 12, core: 2. Of those that a mesh axis runs over, the one named last changes fastest.
Arguments:
- grad_parts: bfloat16 [12, 512, 196608], P('rep', 'shard'), may hold values from -12 to 12
- owner_plan: int32 [12, 32], P('rep'), may hold values from 0 to 63, as said below
- refresh: int32 [12, 16], P('rep'), may hold values from 0 to 63, as said below
- roots: bfloat16 [12, 64, 2, 512, 512], P('rep', 'shard'), may hold values from -0.02 to 0.52
Outputs:
- update: bfloat16 [512, 196608], P('shard', 'rep')
Inputs may be any that keep to these rules, and one draw needn't show every extreme that they name: `owner_plan`: within each replica's row the 32 owners are distinct; otherwise the assignment is arbitrary. `refresh`: entry 2 b + s names side s (0 left, 1 right) of block b of the row's replica; no block appears twice in a row.
All inputs are finite; a program needn't handle non-finite values.
Results may differ from a plain program's by a relative error of at most 0.018.
Values may be sent and summed in bfloat16 or wider, within the bound.
No kernel may reach another device: no remote copies, remote signals or barrier semaphores. Data moves between devices by JAX's collectives and lax.ppermute only.
A program may use at most 32 MiB of HBM per device.

v0:
```python
import functools

import jax
import jax.numpy as jnp
from jax import lax
from jax.experimental import pallas as pl
from jax.experimental.pallas import tpu as pltpu
from jax.sharding import PartitionSpec as P


damping = 0.1

LONG_ARM = {6: 4, 5: 4, 4: 2, 3: 2, 2: 0, 1: 0}
SHORT_ARM = {5: 4, 4: 2, 3: 2, 2: 0, 1: 0}


def steps_before(parent, node):
    children = [c for c in parent if parent[c] == node]
    return 1 + max(steps_before(parent, c) for c in children) if children else 0


def reduce_windows(partial, shards, replicas):
    rows = partial.shape[0]
    width = partial.shape[1] // replicas
    here = lax.axis_index("rep")
    toward = jnp.where(lax.axis_index("shard") % 2 == 0, 1, -1)
    arms = [
        (LONG_ARM, -1, {node: [] for node in range(7)}),
        (SHORT_ARM, 1, {node: [] for node in range(7)}),
    ]

    def own(source, sign, node):
        window = (here + toward * sign * node + replicas) % replicas
        return lax.dynamic_slice(source, (0, window * width), (rows, width))

    def pairs(sign, hops):
        out = []
        for shard in range(shards):
            way = sign if shard % 2 == 0 else -sign
            for z in range(replicas):
                out.append((shard * replicas + z, shard * replicas + (z + way * hops) % replicas))
        return out

    def send(arm, nodes, payload):
        parent, sign, got = arm
        landed = lax.ppermute(payload, ("shard", "rep"), pairs(sign, nodes[0] - parent[nodes[0]]))
        for place, node in enumerate(nodes):
            got[parent[node]].append(landed if len(nodes) == 1 else landed[place])

    def level(parent, step):
        return sorted((n for n in parent if steps_before(parent, n) == step), reverse=True)

    firsts, leaves = [], []
    for arm in arms:
        nodes = level(arm[0], 0)
        chain = [n for n in nodes if arm[0][n] == arm[0][nodes[0]]]
        firsts += [(arm, n) for n in chain]
        leaves.append((arm, [n for n in nodes if n not in chain]))
    slices = [own(partial, arm[1], node) for arm, node in firsts]
    partial, *slices = lax.optimization_barrier((partial, *slices))
    for (arm, node), payload in zip(firsts, slices):
        send(arm, [node], payload)
    last = max(steps_before(parent, node) for parent, _, _ in arms for node in parent)
    held = {(0, 0, 0): own(partial, 1, 0)}
    for index, (parent, sign, _) in enumerate(arms):
        for node in parent:
            if (arms[index], node) not in firsts:
                held[index, node, 0] = own(partial, sign, node)
    held = dict(zip(held, lax.optimization_barrier(tuple(held.values()))))
    for step in range(last + 1):
        todo = []
        for index, arm in enumerate(arms):
            for node in level(arm[0], step) if step else []:
                message = held[index, node, 0]
                for term in arm[2][node]:
                    message = message + term
                todo.append((arm, node, message))
        for index, (arm, nodes) in enumerate(leaves):
            for node in nodes:
                needed = steps_before(arm[0], arm[0][node]) if arm[0][node] else last + 1
                if needed - 2 == step:
                    todo.append((arm, node, held[index, node, 0]))
        if todo:
            payloads = lax.optimization_barrier(tuple(entry[2] for entry in todo))
            for (arm, node, _), payload in zip(todo, payloads):
                send(arm, [node], payload)
    terms = {(0, 0): held[0, 0, 0]}
    return [terms[0, 0]] + [term for _, _, got in arms for term in got[0]]


def dispatch_kernel(terms, owner_ref, *refs):
    term_refs, out_ref = refs[:terms], refs[terms]
    blocks = owner_ref.shape[0]
    width = out_ref.shape[2]
    out_ref[...] = jnp.zeros_like(out_ref)
    for block in range(blocks):
        columns = slice(block * width, (block + 1) * width)
        total = term_refs[0][:, columns].astype(jnp.float32)
        for ref in term_refs[1:]:
            total = total + ref[:, columns].astype(jnp.float32)
        out_ref[owner_ref[block]] = total.astype(jnp.bfloat16)


def mul(first, second):
    return jnp.dot(
        first.astype(jnp.bfloat16), second.astype(jnp.bfloat16), preferred_element_type=jnp.float32
    )


def total_of(values):
    return jnp.sum(jnp.sum(values, axis=0, keepdims=True), axis=1, keepdims=True)


def owner_kernel(me_ref, owner_ref, refresh_ref, grad_ref, roots_ref, out_ref, stat_ref, root_ref):
    size = grad_ref.shape[0]
    me = me_ref[0]
    local_id = jnp.int32(-1)
    for block in range(owner_ref.shape[0]):
        local_id = jnp.where(owner_ref[block] == me, jnp.int32(block), local_id)
    side = jnp.int32(-1)
    for entry in range(refresh_ref.shape[0]):
        value = refresh_ref[entry]
        side = jnp.where(value == 2 * local_id, jnp.int32(0), side)
        side = jnp.where(value == 2 * local_id + 1, jnp.int32(1), side)

    @pl.when(local_id >= 0)
    def _():
        grad = grad_ref[...]
        values = grad.astype(jnp.float32)
        grad_squares = total_of(values * values)

        @pl.when(side != 0)
        def _():
            root_ref[0] = roots_ref[0]

        @pl.when(side != 1)
        def _():
            root_ref[1] = roots_ref[1]

        @pl.when(side == 0)
        def _():
            stat_ref[...] = lax.dot_general(
                grad, grad, (((1,), (1,)), ((), ())), preferred_element_type=jnp.float32
            )

        @pl.when(side == 1)
        def _():
            stat_ref[...] = lax.dot_general(
                grad, grad, (((0,), (0,)), ((), ())), preferred_element_type=jnp.float32
            )

        @pl.when(side >= 0)
        def _():
            rows = lax.broadcasted_iota(jnp.int32, (size, size), 0)
            cols = lax.broadcasted_iota(jnp.int32, (size, size), 1)
            eye = jnp.where(rows == cols, 1.0, 0.0).astype(jnp.float32)
            damped = stat_ref[...] + (damping * grad_squares / size + 1e-06) * eye
            scale = 2.5 / jnp.sqrt(total_of(damped * damped))
            one = damped * scale
            one_low = one.astype(jnp.bfloat16)
            two = mul(one_low, one_low)
            three = mul(two, one_low)
            applied = 1.5625 * one - 0.625 * two + 0.0625 * three
            moment = 1.5625 * applied + mul(0.0625 * two - 0.625 * one, applied)
            root = 1.5625 * eye - 0.3125 * (one + moment) + 0.0625 * mul(one_low, moment)
            root = root * jnp.sqrt(jnp.sqrt(scale))
            root_ref[side] = root.astype(jnp.bfloat16)

        left = jnp.dot(root_ref[0], grad, preferred_element_type=jnp.float32).astype(jnp.bfloat16)
        precon = jnp.dot(left, root_ref[1], preferred_element_type=jnp.float32)
        count = float(size * size)
        graft = jnp.sqrt(
            (grad_squares / count + 1e-06) / (total_of(precon * precon) / count + 1e-06)
        )
        out_ref[...] = (precon * graft).astype(jnp.bfloat16)

    @pl.when(local_id < 0)
    def _():
        out_ref[...] = jnp.zeros_like(out_ref)


def placing_kernel(owner_ref, returned_ref, out_ref):
    width = returned_ref.shape[2]
    for block in range(owner_ref.shape[0]):
        out_ref[:, block * width : (block + 1) * width] = returned_ref[owner_ref[block]]


SMEM = pl.BlockSpec(memory_space=pltpu.SMEM)
VMEM = pl.BlockSpec(memory_space=pltpu.VMEM)


def call(kernel, out_shape, in_specs, scratch, megabytes):
    return pl.pallas_call(
        kernel,
        out_shape=jax.ShapeDtypeStruct(out_shape, jnp.bfloat16),
        in_specs=in_specs,
        out_specs=VMEM,
        scratch_shapes=scratch,
        compiler_params=pltpu.CompilerParams(vmem_limit_bytes=megabytes << 20),
    )


def local(shards, replicas, grad_parts, owner_plan, refresh, roots):
    size = roots.shape[-1]
    rows = grad_parts.shape[1]
    owner_row = owner_plan[0]
    blocks = owner_row.shape[0]
    terms = reduce_windows(grad_parts[0], shards, replicas)
    outgoing = call(
        functools.partial(dispatch_kernel, len(terms)),
        (shards, rows, size),
        [SMEM] + [VMEM] * len(terms),
        [],
        8,
    )(owner_row, *terms)
    incoming = lax.all_to_all(outgoing, "shard", split_axis=0, concat_axis=0, tiled=True)
    update = call(
        owner_kernel,
        (size, size),
        [SMEM, SMEM, SMEM, VMEM, VMEM],
        [pltpu.VMEM((size, size), jnp.float32), pltpu.VMEM((2, size, size), jnp.bfloat16)],
        32,
    )(
        lax.axis_index("shard").astype(jnp.int32)[None],
        owner_row,
        refresh[0],
        incoming.reshape(size, size),
        roots[0, 0],
    )
    returned = lax.all_to_all(
        update.reshape(shards, rows, size), "shard", split_axis=0, concat_axis=0, tiled=True
    )
    return call(placing_kernel, (rows, blocks * size), [SMEM, VMEM], [], 8)(owner_row, returned)


def solution(mesh):
    placed = (
        P("rep", "shard", None),
        P("rep", None),
        P("rep", None),
        P("rep", "shard", None, None, None),
    )
    body = functools.partial(local, mesh.shape["shard"], mesh.shape["rep"])
    return jax.shard_map(
        body, mesh=mesh, in_specs=placed, out_specs=P("shard", "rep"), check_vma=False
    )
```

profile of v0, /device:TPU:1, one launch (start us, length us, event | category | flops | bytes accessed | tf_op | source)
XLA Modules:
  0.0 127.6 jit_solution(11620523072211129261)
XLA Ops:
  0.0 1.2 dynamic-slice_bitcast_fusion
  1.2 6.6 %collective-permute-start = (bf16[8,16384]{1,0:T(8,128)(2,1)S(1)}, bf16[8,16384]{1,0:T(8,128)(2,1)S(1)}, u32[]{:S(2)}, u32[]{:S(2)}) collective-permute-start(bf16[8,16384]{1,0:T(8,128)(2,1)S(1)} %get-tuple-element.29), channel_id=1, source_target_pairs={{0,10},{1,11},{2,0},{3,1},{4,2},{5,3},{6,4},{7,5},{8,6},{9,7},{10,... | collective-permute-start | bytes 786440 | tf_op jit(solution)/shard_map/ppermute | solution.py:46
  7.8 4.0 %collective-permute-start.1 = (bf16[8,16384]{1,0:T(8,128)(2,1)S(1)}, bf16[8,16384]{1,0:T(8,128)(2,1)S(1)}, u32[]{:S(2)}, u32[]{:S(2)}) collective-permute-start(bf16[8,16384]{1,0:T(8,128)(2,1)S(1)} %get-tuple-element.30), channel_id=1, source_target_pairs={{0,11},{1,0},{2,1},{3,2},{4,3},{5,4},{6,5},{7,6},{8,7},{9,8},{10,9... | collective-permute-start | bytes 786440 | tf_op jit(solution)/shard_map/ppermute | solution.py:46
  11.8 8.3 %collective-permute-start.2 = (bf16[8,16384]{1,0:T(8,128)(2,1)S(1)}, bf16[8,16384]{1,0:T(8,128)(2,1)S(1)}, u32[]{:S(2)}, u32[]{:S(2)}) collective-permute-start(bf16[8,16384]{1,0:T(8,128)(2,1)S(1)} %get-tuple-element.32), channel_id=1, source_target_pairs={{0,1},{1,2},{2,3},{3,4},{4,5},{5,6},{6,7},{7,8},{8,9},{9,10},{10,1... | collective-permute-start | bytes 786440 | tf_op jit(solution)/shard_map/ppermute | solution.py:46
  20.4 1.8 %constant_dynamic-slice_fusion = (bf16[8,16384]{1,0:T(8,128)(2,1)S(1)}, bf16[8,16384]{1,0:T(8,128)(2,1)S(1)}, bf16[8,16384]{1,0:T(8,128)(2,1)S(1)}, bf16[8,16384...) fusion(bf16[8,196608]{1,0:T(8,128)(2,1)} %bitcast.20, ...), kind=kLoop, calls=%fused_computation.6 | loop fusion | bytes 4718628 | tf_op jit(solution)/shard_map/dynamic_slice | solution.py:34
  22.1 0.0 copy-start.1
  22.1 1.9 %collective-permute-start.4 = (bf16[8,16384]{1,0:T(8,128)(2,1)S(1)}, bf16[8,16384]{1,0:T(8,128)(2,1)S(1)}, u32[]{:S(2)}, u32[]{:S(2)}) collective-permute-start(bf16[8,16384]{1,0:T(8,128)(2,1)S(1)} %get-tuple-element.39), channel_id=1, source_target_pairs={{0,11},{1,0},{2,1},{3,2},{4,3},{5,4},{6,5},{7,6},{8,7},{9,8},{10,9... | collective-permute-start | bytes 786440 | tf_op jit(solution)/shard_map/ppermute | solution.py:46
  24.1 4.4 %collective-permute-done.2 = bf16[8,16384]{1,0:T(8,128)(2,1)S(1)} collective-permute-done((bf16[8,16384]{1,0:T(8,128)(2,1)S(1)}, bf16[8,16384]{1,0:T(8,128)(2,1)S(1)}, u32[]{:S(2)}, u32[]{:S(2)}) %collective-permute-start.2) | collective-permute-done | bytes 262176 | tf_op jit(solution)/shard_map/ppermute | solution.py:46
  28.5 0.1 add.216
  28.6 0.0 copy-start
  28.6 0.0 copy-start.2
  28.6 0.0 collective-permute-done
  28.6 0.0 collective-permute-done.1
  28.6 2.1 %collective-permute-start.5 = (bf16[8,16384]{1,0:T(8,128)(2,1)S(1)}, bf16[8,16384]{1,0:T(8,128)(2,1)S(1)}, u32[]{:S(2)}, u32[]{:S(2)}) collective-permute-start(bf16[8,16384]{1,0:T(8,128)(2,1)S(1)} %add_add_fusion.2), channel_id=1, source_target_pairs={{0,10},{1,11},{2,0},{3,1},{4,2},{5,3},{6,4},{7,5},{8,6},{9,7},{10,... | collective-permute-start | bytes 786440 | tf_op jit(solution)/shard_map/ppermute | solution.py:46
  30.7 5.3 %collective-permute-start.6 = (bf16[8,16384]{1,0:T(8,128)(2,1)S(1)}, bf16[8,16384]{1,0:T(8,128)(2,1)S(1)}, u32[]{:S(2)}, u32[]{:S(2)}) collective-permute-start(bf16[8,16384]{1,0:T(8,128)(2,1)S(1)} %get-tuple-element.42), channel_id=1, source_target_pairs={{0,1},{1,2},{2,3},{3,4},{4,5},{5,6},{6,7},{7,8},{8,9},{9,10},{10,1... | collective-permute-start | bytes 786440 | tf_op jit(solution)/shard_map/ppermute | solution.py:46
  36.0 1.9 %collective-permute-start.3 = (bf16[8,16384]{1,0:T(8,128)(2,1)S(1)}, bf16[8,16384]{1,0:T(8,128)(2,1)S(1)}, u32[]{:S(2)}, u32[]{:S(2)}) collective-permute-start(bf16[8,16384]{1,0:T(8,128)(2,1)S(1)} %get-tuple-element.35), channel_id=1, source_target_pairs={{0,11},{1,0},{2,1},{3,2},{4,3},{5,4},{6,5},{7,6},{8,7},{9,8},{10,9... | collective-permute-start | bytes 786440 | tf_op jit(solution)/shard_map/ppermute | solution.py:46
  38.0 4.3 %collective-permute-start.7 = (bf16[8,16384]{1,0:T(8,128)(2,1)S(1)}, bf16[8,16384]{1,0:T(8,128)(2,1)S(1)}, u32[]{:S(2)}, u32[]{:S(2)}) collective-permute-start(bf16[8,16384]{1,0:T(8,128)(2,1)S(1)} %add.216), channel_id=1, source_target_pairs={{0,2},{1,3},{2,4},{3,5},{4,6},{5,7},{6,8},{7,9},{8,10},{9,11},{10,... | collective-permute-start | bytes 786440 | tf_op jit(solution)/shard_map/ppermute | solution.py:46
  42.2 0.0 collective-permute-done.4
  42.2 3.4 %collective-permute-start.9 = (bf16[8,16384]{1,0:T(8,128)(2,1)S(1)}, bf16[8,16384]{1,0:T(8,128)(2,1)S(1)}, u32[]{:S(2)}, u32[]{:S(2)}) collective-permute-start(bf16[8,16384]{1,0:T(8,128)(2,1)S(1)} %get-tuple-element.45), channel_id=1, source_target_pairs={{0,1},{1,2},{2,3},{3,4},{4,5},{5,6},{6,7},{7,8},{8,9},{9,10},{10,1... | collective-permute-start | bytes 786440 | tf_op jit(solution)/shard_map/ppermute | solution.py:46
  45.6 0.0 collective-permute-done.5
  45.7 0.0 collective-permute-done.6
  45.7 6.6 %collective-permute-done.7 = bf16[8,16384]{1,0:T(8,128)(2,1)S(1)} collective-permute-done((bf16[8,16384]{1,0:T(8,128)(2,1)S(1)}, bf16[8,16384]{1,0:T(8,128)(2,1)S(1)}, u32[]{:S(2)}, u32[]{:S(2)}) %collective-permute-start.7) | collective-permute-done | bytes 262176 | tf_op jit(solution)/shard_map/ppermute | solution.py:46
  52.3 5.0 %collective-permute-start.8 = (bf16[8,16384]{1,0:T(8,128)(2,1)S(1)}, bf16[8,16384]{1,0:T(8,128)(2,1)S(1)}, u32[]{:S(2)}, u32[]{:S(2)}) collective-permute-start(bf16[8,16384]{1,0:T(8,128)(2,1)S(1)} %add_add_fusion.1), channel_id=1, source_target_pairs={{0,10},{1,11},{2,0},{3,1},{4,2},{5,3},{6,4},{7,5},{8,6},{9,7},{10,... | collective-permute-start | bytes 786440 | tf_op jit(solution)/shard_map/ppermute | solution.py:46
  57.4 2.9 %collective-permute-start.10 = (bf16[8,16384]{1,0:T(8,128)(2,1)S(1)}, bf16[8,16384]{1,0:T(8,128)(2,1)S(1)}, u32[]{:S(2)}, u32[]{:S(2)}) collective-permute-start(bf16[8,16384]{1,0:T(8,128)(2,1)S(1)} %add_add_fusion), channel_id=1, source_target_pairs={{0,2},{1,3},{2,4},{3,5},{4,6},{5,7},{6,8},{7,9},{8,10},{9,11},{10,... | collective-permute-start | bytes 786440 | tf_op jit(solution)/shard_map/ppermute | solution.py:46
  60.3 0.0 collective-permute-done.3.refs_1_
  60.3 0.0 collective-permute-done.9.refs_3_
  60.3 9.5 %collective-permute-done.8.refs_2_ = bf16[8,16384]{1,0:T(8,128)(2,1)S(1)} collective-permute-done((bf16[8,16384]{1,0:T(8,128)(2,1)S(1)}, bf16[8,16384]{1,0:T(8,128)(2,1)S(1)}, u32[]{:S(2)}, u32[]{:S(2)}) %collective-permute-start.8) | collective-permute-done | bytes 262176 | tf_op jit(solution)/shard_map/ppermute | solution.py:46
  69.8 1.0 collective-permute-done.10.refs_4_
  70.8 0.0 copy-done.1
  70.8 0.7 shard_map.46
  71.5 28.0 %all_to_all.10 = bf16[64,8,512]{2,1,0:T(8,128)(2,1)S(1)} all-to-all(bf16[64,8,512]{2,1,0:T(8,128)(2,1)S(1)} %shard_map.46), channel_id=1, replica_groups=mesh['shard'=64,'rep'=12] {'shard'}, dimensions={0} | all-to-all | bytes 1048576 | tf_op jit(solution)/shard_map/all_to_all | solution.py:216
  99.5 0.0 copy-done
  99.5 0.0 copy-done.2
  99.5 0.6 shard_map.47
  100.1 26.2 %all_to_all.11.returned_ref = bf16[64,8,512]{2,1,0:T(8,128)(2,1)S(1)} all-to-all(bf16[64,8,512]{2,1,0:T(8,128)(2,1)S(1)} %bitcast.14), channel_id=1, replica_groups=mesh['shard'=64,'rep'=12] {'shard'}, dimensions={0} | all-to-all | bytes 1048576 | tf_op jit(solution)/shard_map/all_to_all | solution.py:230
  126.4 1.3 shard_map.48
  (3 shorter events, 0.1 us)
Async XLA Ops:
  1.2 27.4 %collective-permute-start = (bf16[8,16384]{1,0:T(8,128)(2,1)S(1)}, bf16[8,16384]{1,0:T(8,128)(2,1)S(1)}, u32[]{:S(2)}, u32[]{:S(2)}) collective-permute-start(bf16[8,16384]{1,0:T(8,128)(2,1)S(1)} %get-tuple-element.29), channel_id=1, source_target_pairs={{0,10},{1,11},{2,0},{3,1},{4,2},{5,3},{6,4},{7,5},{8,6},{9,7},{10,... | collective-permute-start | bytes 786440 | tf_op jit(solution)/shard_map/ppermute | solution.py:46
  7.8 20.8 %collective-permute-start.1 = (bf16[8,16384]{1,0:T(8,128)(2,1)S(1)}, bf16[8,16384]{1,0:T(8,128)(2,1)S(1)}, u32[]{:S(2)}, u32[]{:S(2)}) collective-permute-start(bf16[8,16384]{1,0:T(8,128)(2,1)S(1)} %get-tuple-element.30), channel_id=1, source_target_pairs={{0,11},{1,0},{2,1},{3,2},{4,3},{5,4},{6,5},{7,6},{8,7},{9,8},{10,9... | collective-permute-start | bytes 786440 | tf_op jit(solution)/shard_map/ppermute | solution.py:46
  11.8 16.7 %collective-permute-start.2 = (bf16[8,16384]{1,0:T(8,128)(2,1)S(1)}, bf16[8,16384]{1,0:T(8,128)(2,1)S(1)}, u32[]{:S(2)}, u32[]{:S(2)}) collective-permute-start(bf16[8,16384]{1,0:T(8,128)(2,1)S(1)} %get-tuple-element.32), channel_id=1, source_target_pairs={{0,1},{1,2},{2,3},{3,4},{4,5},{5,6},{6,7},{7,8},{8,9},{9,10},{10,1... | collective-permute-start | bytes 786440 | tf_op jit(solution)/shard_map/ppermute | solution.py:46
  22.1 48.7 %copy-start.1 = (s32[1,32]{1,0:T(1,128)S(1)}, s32[1,32]{1,0:T(1,128)}, u32[]{:S(2)}) copy-start(s32[1,32]{1,0:T(1,128)} %param.5) | copy-start | bytes 388
  22.1 20.1 %collective-permute-start.4 = (bf16[8,16384]{1,0:T(8,128)(2,1)S(1)}, bf16[8,16384]{1,0:T(8,128)(2,1)S(1)}, u32[]{:S(2)}, u32[]{:S(2)}) collective-permute-start(bf16[8,16384]{1,0:T(8,128)(2,1)S(1)} %get-tuple-element.39), channel_id=1, source_target_pairs={{0,11},{1,0},{2,1},{3,2},{4,3},{5,4},{6,5},{7,6},{8,7},{9,8},{10,9... | collective-permute-start | bytes 786440 | tf_op jit(solution)/shard_map/ppermute | solution.py:46
  28.6 71.0 %copy-start = (bf16[1,1,2,512,512]{4,3,2,1,0:T(8,128)(2,1)S(1)}, bf16[1,1,2,512,512]{4,3,2,1,0:T(8,128)(2,1)}, u32[]{:S(2)}) copy-start(bf16[1,1,2,512,512]{4,3,2,1,0:T(8,128)(2,1)} %param.7) | copy-start | bytes 3145732
  28.6 70.9 %copy-start.2 = (s32[1,16]{1,0:T(1,128)S(1)}, s32[1,16]{1,0:T(1,128)}, u32[]{:S(2)}) copy-start(s32[1,16]{1,0:T(1,128)} %param.6) | copy-start | bytes 196
  28.6 17.0 %collective-permute-start.5 = (bf16[8,16384]{1,0:T(8,128)(2,1)S(1)}, bf16[8,16384]{1,0:T(8,128)(2,1)S(1)}, u32[]{:S(2)}, u32[]{:S(2)}) collective-permute-start(bf16[8,16384]{1,0:T(8,128)(2,1)S(1)} %add_add_fusion.2), channel_id=1, source_target_pairs={{0,10},{1,11},{2,0},{3,1},{4,2},{5,3},{6,4},{7,5},{8,6},{9,7},{10,... | collective-permute-start | bytes 786440 | tf_op jit(solution)/shard_map/ppermute | solution.py:46
  30.7 15.0 %collective-permute-start.6 = (bf16[8,16384]{1,0:T(8,128)(2,1)S(1)}, bf16[8,16384]{1,0:T(8,128)(2,1)S(1)}, u32[]{:S(2)}, u32[]{:S(2)}) collective-permute-start(bf16[8,16384]{1,0:T(8,128)(2,1)S(1)} %get-tuple-element.42), channel_id=1, source_target_pairs={{0,1},{1,2},{2,3},{3,4},{4,5},{5,6},{6,7},{7,8},{8,9},{9,10},{10,1... | collective-permute-start | bytes 786440 | tf_op jit(solution)/shard_map/ppermute | solution.py:46
  36.0 24.2 %collective-permute-start.3 = (bf16[8,16384]{1,0:T(8,128)(2,1)S(1)}, bf16[8,16384]{1,0:T(8,128)(2,1)S(1)}, u32[]{:S(2)}, u32[]{:S(2)}) collective-permute-start(bf16[8,16384]{1,0:T(8,128)(2,1)S(1)} %get-tuple-element.35), channel_id=1, source_target_pairs={{0,11},{1,0},{2,1},{3,2},{4,3},{5,4},{6,5},{7,6},{8,7},{9,8},{10,9... | collective-permute-start | bytes 786440 | tf_op jit(solution)/shard_map/ppermute | solution.py:46
  38.0 14.3 %collective-permute-start.7 = (bf16[8,16384]{1,0:T(8,128)(2,1)S(1)}, bf16[8,16384]{1,0:T(8,128)(2,1)S(1)}, u32[]{:S(2)}, u32[]{:S(2)}) collective-permute-start(bf16[8,16384]{1,0:T(8,128)(2,1)S(1)} %add.216), channel_id=1, source_target_pairs={{0,2},{1,3},{2,4},{3,5},{4,6},{5,7},{6,8},{7,9},{8,10},{9,11},{10,... | collective-permute-start | bytes 786440 | tf_op jit(solution)/shard_map/ppermute | solution.py:46
  42.2 18.0 %collective-permute-start.9 = (bf16[8,16384]{1,0:T(8,128)(2,1)S(1)}, bf16[8,16384]{1,0:T(8,128)(2,1)S(1)}, u32[]{:S(2)}, u32[]{:S(2)}) collective-permute-start(bf16[8,16384]{1,0:T(8,128)(2,1)S(1)} %get-tuple-element.45), channel_id=1, source_target_pairs={{0,1},{1,2},{2,3},{3,4},{4,5},{5,6},{6,7},{7,8},{8,9},{9,10},{10,1... | collective-permute-start | bytes 786440 | tf_op jit(solution)/shard_map/ppermute | solution.py:46
  52.3 17.5 %collective-permute-start.8 = (bf16[8,16384]{1,0:T(8,128)(2,1)S(1)}, bf16[8,16384]{1,0:T(8,128)(2,1)S(1)}, u32[]{:S(2)}, u32[]{:S(2)}) collective-permute-start(bf16[8,16384]{1,0:T(8,128)(2,1)S(1)} %add_add_fusion.1), channel_id=1, source_target_pairs={{0,10},{1,11},{2,0},{3,1},{4,2},{5,3},{6,4},{7,5},{8,6},{9,7},{10,... | collective-permute-start | bytes 786440 | tf_op jit(solution)/shard_map/ppermute | solution.py:46
  57.4 13.5 %collective-permute-start.10 = (bf16[8,16384]{1,0:T(8,128)(2,1)S(1)}, bf16[8,16384]{1,0:T(8,128)(2,1)S(1)}, u32[]{:S(2)}, u32[]{:S(2)}) collective-permute-start(bf16[8,16384]{1,0:T(8,128)(2,1)S(1)} %add_add_fusion), channel_id=1, source_target_pairs={{0,2},{1,3},{2,4},{3,5},{4,6},{5,7},{6,8},{7,9},{8,10},{9,11},{10,... | collective-permute-start | bytes 786440 | tf_op jit(solution)/shard_map/ppermute | solution.py:46
where the time goes:
time: 128 us
  blocking collectives  54.2 us (42%)
  starting transfers between devices  45.7 us (36%)
  waiting for transfers between devices  21.5 us (17%)
  local copies, waits for them, and re-layouts  2.94 us (2%)
  Pallas kernels  2.62 us (2%)
    ppermute x11, starting transfers between devices, send(): lax.ppermute(payload, ('shard', 'rep'), pairs(sign, nodes[0] - parent[nod...  45.7 us
    all_to_all x1, blocking collectives, local(): lax.all_to_all(outgoing, 'shard', split_axis=0, concat_axis=0, tiled=True)  28 us
    all_to_all x1, blocking collectives, local(): lax.all_to_all(update.reshape(shards, rows, size), 'shard', split_axis=0,...  26.2 us
    ppermute x11, waiting for transfers between devices, send(): lax.ppermute(payload, ('shard', 'rep'), pairs(sign, nodes[0] - parent[nod...  21.5 us
    dynamic_slice x2, local copies, waits for them, and re-layouts, own(): return lax.dynamic_slice(source, (0, window * width), (rows, width))  2.92 us
  transfers between devices with their start and end apart: 11, of which 4 were waited for; matrix products, arithmetic and copies ran while one was open for 2% of the time, Pallas kernels for 0%

commit v1 on v0

--- a/solution.py
+++ b/solution.py
@@ -9,6 +9,17 @@
 
 
 damping = 0.1
+
+NEWTON = (
+    25 / 16,
+    -5 / 16 - 3125 / 4096,
+    3125 / 4096,
+    -1250 / 4096,
+    250 / 4096,
+    -25 / 4096,
+    1 / 4096,
+)
+STRIP = 64
 
 LONG_ARM = {6: 4, 5: 4, 4: 2, 3: 2, 2: 0, 1: 0}
 SHORT_ARM = {5: 4, 4: 2, 3: 2, 2: 0, 1: 0}
@@ -92,7 +103,6 @@
     term_refs, out_ref = refs[:terms], refs[terms]
     blocks = owner_ref.shape[0]
     width = out_ref.shape[2]
-    out_ref[...] = jnp.zeros_like(out_ref)
     for block in range(blocks):
         columns = slice(block * width, (block + 1) * width)
         total = term_refs[0][:, columns].astype(jnp.float32)
@@ -102,16 +112,24 @@
 
 
 def mul(first, second):
-    return jnp.dot(
-        first.astype(jnp.bfloat16), second.astype(jnp.bfloat16), preferred_element_type=jnp.float32
-    )
-
-
-def total_of(values):
-    return jnp.sum(jnp.sum(values, axis=0, keepdims=True), axis=1, keepdims=True)
-
-
-def owner_kernel(me_ref, owner_ref, refresh_ref, grad_ref, roots_ref, out_ref, stat_ref, root_ref):
+    return jnp.dot(first, second, preferred_element_type=jnp.float32)
+
+
+def strips(size):
+    return [slice(start, start + STRIP) for start in range(0, size, STRIP)]
+
+
+def sum_of_squares(size, strip_of):
+    total = 0.0
+    for strip in strips(size):
+        values = strip_of(strip)
+        total = total + jnp.sum((values * values).reshape(STRIP // 8, 8, size), axis=0)
+    return jnp.sum(jnp.sum(total, axis=0, keepdims=True), axis=1, keepdims=True)
+
+
+def owner_kernel(
+    me_ref, owner_ref, refresh_ref, grad_ref, roots_ref, out_ref, one_ref, two_ref, three_ref, low_ref, root_ref
+):
     size = grad_ref.shape[0]
     me = me_ref[0]
     local_id = jnp.int32(-1)
@@ -123,11 +141,14 @@
         side = jnp.where(value == 2 * local_id, jnp.int32(0), side)
         side = jnp.where(value == 2 * local_id + 1, jnp.int32(1), side)
 
+    def diagonal(strip, value):
+        rows = lax.broadcasted_iota(jnp.int32, (STRIP, size), 0) + strip.start
+        cols = lax.broadcasted_iota(jnp.int32, (STRIP, size), 1)
+        return jnp.where(rows == cols, value, 0.0)
+
     @pl.when(local_id >= 0)
     def _():
-        grad = grad_ref[...]
-        values = grad.astype(jnp.float32)
-        grad_squares = total_of(values * values)
+        grad_squares = sum_of_squares(size, lambda strip: grad_ref[strip].astype(jnp.float32))
 
         @pl.when(side != 0)
         def _():
@@ -139,40 +160,58 @@
 
         @pl.when(side == 0)
         def _():
-            stat_ref[...] = lax.dot_general(
-                grad, grad, (((1,), (1,)), ((), ())), preferred_element_type=jnp.float32
+            one_ref[...] = lax.dot_general(
+                grad_ref[...],
+                grad_ref[...],
+                (((1,), (1,)), ((), ())),
+                preferred_element_type=jnp.float32,
             )
 
         @pl.when(side == 1)
         def _():
-            stat_ref[...] = lax.dot_general(
-                grad, grad, (((0,), (0,)), ((), ())), preferred_element_type=jnp.float32
+            one_ref[...] = lax.dot_general(
+                grad_ref[...],
+                grad_ref[...],
+                (((0,), (0,)), ((), ())),
+                preferred_element_type=jnp.float32,
             )
 
         @pl.when(side >= 0)
         def _():
-            rows = lax.broadcasted_iota(jnp.int32, (size, size), 0)
-            cols = lax.broadcasted_iota(jnp.int32, (size, size), 1)
-            eye = jnp.where(rows == cols, 1.0, 0.0).astype(jnp.float32)
-            damped = stat_ref[...] + (damping * grad_squares / size + 1e-06) * eye
-            scale = 2.5 / jnp.sqrt(total_of(damped * damped))
-            one = damped * scale
-            one_low = one.astype(jnp.bfloat16)
-            two = mul(one_low, one_low)
-            three = mul(two, one_low)
-            applied = 1.5625 * one - 0.625 * two + 0.0625 * three
-            moment = 1.5625 * applied + mul(0.0625 * two - 0.625 * one, applied)
-            root = 1.5625 * eye - 0.3125 * (one + moment) + 0.0625 * mul(one_low, moment)
-            root = root * jnp.sqrt(jnp.sqrt(scale))
-            root_ref[side] = root.astype(jnp.bfloat16)
-
-        left = jnp.dot(root_ref[0], grad, preferred_element_type=jnp.float32).astype(jnp.bfloat16)
-        precon = jnp.dot(left, root_ref[1], preferred_element_type=jnp.float32)
+            ridge = damping * grad_squares / size + 1e-06
+            norm = sum_of_squares(size, lambda strip: one_ref[strip] + diagonal(strip, ridge))
+            scale = 2.5 / jnp.sqrt(norm)
+            for strip in strips(size):
+                one = (one_ref[strip] + diagonal(strip, ridge)) * scale
+                one_ref[strip] = one
+                low_ref[0, strip] = one.astype(jnp.bfloat16)
+            two_ref[...] = mul(low_ref[0], low_ref[0])
+            for strip in strips(size):
+                low_ref[1, strip] = two_ref[strip].astype(jnp.bfloat16)
+            three_ref[...] = mul(low_ref[1], low_ref[0])
+            for strip in strips(size):
+                one, two, three = one_ref[strip], two_ref[strip], three_ref[strip]
+                high = NEWTON[4] * one + NEWTON[5] * two + NEWTON[6] * three
+                low_ref[0, strip] = three.astype(jnp.bfloat16)
+                low_ref[1, strip] = high.astype(jnp.bfloat16)
+                rest = NEWTON[1] * one + NEWTON[2] * two + NEWTON[3] * three
+                one_ref[strip] = rest + diagonal(strip, NEWTON[0])
+            two_ref[...] = mul(low_ref[0], low_ref[1])
+            fourth = jnp.sqrt(jnp.sqrt(scale))
+            for strip in strips(size):
+                root_ref[side, strip] = ((two_ref[strip] + one_ref[strip]) * fourth).astype(
+                    jnp.bfloat16
+                )
+
+        two_ref[...] = mul(root_ref[0], grad_ref[...])
+        for strip in strips(size):
+            low_ref[0, strip] = two_ref[strip].astype(jnp.bfloat16)
+        one_ref[...] = mul(low_ref[0], root_ref[1])
         count = float(size * size)
-        graft = jnp.sqrt(
-            (grad_squares / count + 1e-06) / (total_of(precon * precon) / count + 1e-06)
-        )
-        out_ref[...] = (precon * graft).astype(jnp.bfloat16)
+        precon_squares = sum_of_squares(size, lambda strip: one_ref[strip])
+        graft = jnp.sqrt((grad_squares / count + 1e-06) / (precon_squares / count + 1e-06))
+        for strip in strips(size):
+            out_ref[strip] = (one_ref[strip] * graft).astype(jnp.bfloat16)
 
     @pl.when(local_id < 0)
     def _():
@@ -218,7 +257,7 @@
         owner_kernel,
         (size, size),
         [SMEM, SMEM, SMEM, VMEM, VMEM],
-        [pltpu.VMEM((size, size), jnp.float32), pltpu.VMEM((2, size, size), jnp.bfloat16)],
+        [pltpu.VMEM((size, size), jnp.float32)] * 3 + [pltpu.VMEM((2, size, size), jnp.bfloat16)] * 2,
         32,
     )(
         lax.axis_index("shard").astype(jnp.int32)[None],

time: 128 us -> 128 us (level)
  no operation moved by 1% of the time
where the time goes in v1:
time: 128 us; the launch traced here: 127 us
  blocking collectives  54 us (42%)
  starting transfers between devices  45.7 us (36%)
  waiting for transfers between devices  21.5 us (17%)
  local copies, waits for them, and re-layouts  2.94 us (2%)
  Pallas kernels  2.6 us (2%)
    ppermute x11, starting transfers between devices, send(): lax.ppermute(payload, ('shard', 'rep'), pairs(sign, nodes[0] - parent[nod...  45.7 us
    all_to_all x1, blocking collectives, local(): lax.all_to_all(outgoing, 'shard', split_axis=0, concat_axis=0, tiled=True)  28 us
    all_to_all x1, blocking collectives, local(): lax.all_to_all(update.reshape(shards, rows, size), 'shard', split_axis=0,...  26 us
    ppermute x11, waiting for transfers between devices, send(): lax.ppermute(payload, ('shard', 'rep'), pairs(sign, nodes[0] - parent[nod...  21.5 us
    dynamic_slice x2, local copies, waits for them, and re-layouts, own(): return lax.dynamic_slice(source, (0, window * width), (rows, width))  2.92 us
  transfers between devices with their start and end apart: 11, of which 4 were waited for; matrix products, arithmetic and copies ran while one was open for 2% of the time, Pallas kernels for 0%

profile of v1, /device:TPU:1, one launch (start us, length us, event | category | flops | bytes accessed | tf_op | source)
XLA Modules:
  0.0 127.4 jit_solution(16527130624301122626)
XLA Ops:
  0.0 1.2 dynamic-slice_bitcast_fusion
  1.2 6.6 %collective-permute-start = (bf16[8,16384]{1,0:T(8,128)(2,1)S(1)}, bf16[8,16384]{1,0:T(8,128)(2,1)S(1)}, u32[]{:S(2)}, u32[]{:S(2)}) collective-permute-start(bf16[8,16384]{1,0:T(8,128)(2,1)S(1)} %get-tuple-element.29), channel_id=1, source_target_pairs={{0,10},{1,11},{2,0},{3,1},{4,2},{5,3},{6,4},{7,5},{8,6},{9,7},{10,... | collective-permute-start | bytes 786440 | tf_op jit(solution)/shard_map/ppermute | solution.py:57
  7.8 4.0 %collective-permute-start.1 = (bf16[8,16384]{1,0:T(8,128)(2,1)S(1)}, bf16[8,16384]{1,0:T(8,128)(2,1)S(1)}, u32[]{:S(2)}, u32[]{:S(2)}) collective-permute-start(bf16[8,16384]{1,0:T(8,128)(2,1)S(1)} %get-tuple-element.30), channel_id=1, source_target_pairs={{0,11},{1,0},{2,1},{3,2},{4,3},{5,4},{6,5},{7,6},{8,7},{9,8},{10,9... | collective-permute-start | bytes 786440 | tf_op jit(solution)/shard_map/ppermute | solution.py:57
  11.8 8.3 %collective-permute-start.2 = (bf16[8,16384]{1,0:T(8,128)(2,1)S(1)}, bf16[8,16384]{1,0:T(8,128)(2,1)S(1)}, u32[]{:S(2)}, u32[]{:S(2)}) collective-permute-start(bf16[8,16384]{1,0:T(8,128)(2,1)S(1)} %get-tuple-element.32), channel_id=1, source_target_pairs={{0,1},{1,2},{2,3},{3,4},{4,5},{5,6},{6,7},{7,8},{8,9},{9,10},{10,1... | collective-permute-start | bytes 786440 | tf_op jit(solution)/shard_map/ppermute | solution.py:57
  20.4 1.8 %constant_dynamic-slice_fusion = (bf16[8,16384]{1,0:T(8,128)(2,1)S(1)}, bf16[8,16384]{1,0:T(8,128)(2,1)S(1)}, bf16[8,16384]{1,0:T(8,128)(2,1)S(1)}, bf16[8,16384...) fusion(bf16[8,196608]{1,0:T(8,128)(2,1)} %bitcast.20, ...), kind=kLoop, calls=%fused_computation.6 | loop fusion | bytes 4718628 | tf_op jit(solution)/shard_map/dynamic_slice | solution.py:45
  22.1 0.0 copy-start.1
  22.1 1.9 %collective-permute-start.4 = (bf16[8,16384]{1,0:T(8,128)(2,1)S(1)}, bf16[8,16384]{1,0:T(8,128)(2,1)S(1)}, u32[]{:S(2)}, u32[]{:S(2)}) collective-permute-start(bf16[8,16384]{1,0:T(8,128)(2,1)S(1)} %get-tuple-element.39), channel_id=1, source_target_pairs={{0,11},{1,0},{2,1},{3,2},{4,3},{5,4},{6,5},{7,6},{8,7},{9,8},{10,9... | collective-permute-start | bytes 786440 | tf_op jit(solution)/shard_map/ppermute | solution.py:57
  24.1 4.4 %collective-permute-done.2 = bf16[8,16384]{1,0:T(8,128)(2,1)S(1)} collective-permute-done((bf16[8,16384]{1,0:T(8,128)(2,1)S(1)}, bf16[8,16384]{1,0:T(8,128)(2,1)S(1)}, u32[]{:S(2)}, u32[]{:S(2)}) %collective-permute-start.2) | collective-permute-done | bytes 262176 | tf_op jit(solution)/shard_map/ppermute | solution.py:57
  28.5 0.1 add.216
  28.6 0.0 copy-start
  28.6 0.0 copy-start.2
  28.6 0.0 collective-permute-done
  28.6 0.0 collective-permute-done.1
  28.6 2.1 %collective-permute-start.5 = (bf16[8,16384]{1,0:T(8,128)(2,1)S(1)}, bf16[8,16384]{1,0:T(8,128)(2,1)S(1)}, u32[]{:S(2)}, u32[]{:S(2)}) collective-permute-start(bf16[8,16384]{1,0:T(8,128)(2,1)S(1)} %add_add_fusion.2), channel_id=1, source_target_pairs={{0,10},{1,11},{2,0},{3,1},{4,2},{5,3},{6,4},{7,5},{8,6},{9,7},{10,... | collective-permute-start | bytes 786440 | tf_op jit(solution)/shard_map/ppermute | solution.py:57
  30.7 5.3 %collective-permute-start.6 = (bf16[8,16384]{1,0:T(8,128)(2,1)S(1)}, bf16[8,16384]{1,0:T(8,128)(2,1)S(1)}, u32[]{:S(2)}, u32[]{:S(2)}) collective-permute-start(bf16[8,16384]{1,0:T(8,128)(2,1)S(1)} %get-tuple-element.42), channel_id=1, source_target_pairs={{0,1},{1,2},{2,3},{3,4},{4,5},{5,6},{6,7},{7,8},{8,9},{9,10},{10,1... | collective-permute-start | bytes 786440 | tf_op jit(solution)/shard_map/ppermute | solution.py:57
  36.0 1.9 %collective-permute-start.3 = (bf16[8,16384]{1,0:T(8,128)(2,1)S(1)}, bf16[8,16384]{1,0:T(8,128)(2,1)S(1)}, u32[]{:S(2)}, u32[]{:S(2)}) collective-permute-start(bf16[8,16384]{1,0:T(8,128)(2,1)S(1)} %get-tuple-element.35), channel_id=1, source_target_pairs={{0,11},{1,0},{2,1},{3,2},{4,3},{5,4},{6,5},{7,6},{8,7},{9,8},{10,9... | collective-permute-start | bytes 786440 | tf_op jit(solution)/shard_map/ppermute | solution.py:57
  38.0 4.3 %collective-permute-start.7 = (bf16[8,16384]{1,0:T(8,128)(2,1)S(1)}, bf16[8,16384]{1,0:T(8,128)(2,1)S(1)}, u32[]{:S(2)}, u32[]{:S(2)}) collective-permute-start(bf16[8,16384]{1,0:T(8,128)(2,1)S(1)} %add.216), channel_id=1, source_target_pairs={{0,2},{1,3},{2,4},{3,5},{4,6},{5,7},{6,8},{7,9},{8,10},{9,11},{10,... | collective-permute-start | bytes 786440 | tf_op jit(solution)/shard_map/ppermute | solution.py:57
  42.2 0.0 collective-permute-done.4
  42.2 3.4 %collective-permute-start.9 = (bf16[8,16384]{1,0:T(8,128)(2,1)S(1)}, bf16[8,16384]{1,0:T(8,128)(2,1)S(1)}, u32[]{:S(2)}, u32[]{:S(2)}) collective-permute-start(bf16[8,16384]{1,0:T(8,128)(2,1)S(1)} %get-tuple-element.45), channel_id=1, source_target_pairs={{0,1},{1,2},{2,3},{3,4},{4,5},{5,6},{6,7},{7,8},{8,9},{9,10},{10,1... | collective-permute-start | bytes 786440 | tf_op jit(solution)/shard_map/ppermute | solution.py:57
  45.6 0.0 collective-permute-done.5
  45.7 0.0 collective-permute-done.6
  45.7 6.6 %collective-permute-done.7 = bf16[8,16384]{1,0:T(8,128)(2,1)S(1)} collective-permute-done((bf16[8,16384]{1,0:T(8,128)(2,1)S(1)}, bf16[8,16384]{1,0:T(8,128)(2,1)S(1)}, u32[]{:S(2)}, u32[]{:S(2)}) %collective-permute-start.7) | collective-permute-done | bytes 262176 | tf_op jit(solution)/shard_map/ppermute | solution.py:57
  52.3 5.0 %collective-permute-start.8 = (bf16[8,16384]{1,0:T(8,128)(2,1)S(1)}, bf16[8,16384]{1,0:T(8,128)(2,1)S(1)}, u32[]{:S(2)}, u32[]{:S(2)}) collective-permute-start(bf16[8,16384]{1,0:T(8,128)(2,1)S(1)} %add_add_fusion.1), channel_id=1, source_target_pairs={{0,10},{1,11},{2,0},{3,1},{4,2},{5,3},{6,4},{7,5},{8,6},{9,7},{10,... | collective-permute-start | bytes 786440 | tf_op jit(solution)/shard_map/ppermute | solution.py:57
  57.4 2.9 %collective-permute-start.10 = (bf16[8,16384]{1,0:T(8,128)(2,1)S(1)}, bf16[8,16384]{1,0:T(8,128)(2,1)S(1)}, u32[]{:S(2)}, u32[]{:S(2)}) collective-permute-start(bf16[8,16384]{1,0:T(8,128)(2,1)S(1)} %add_add_fusion), channel_id=1, source_target_pairs={{0,2},{1,3},{2,4},{3,5},{4,6},{5,7},{6,8},{7,9},{8,10},{9,11},{10,... | collective-permute-start | bytes 786440 | tf_op jit(solution)/shard_map/ppermute | solution.py:57
  60.3 0.0 collective-permute-done.3.refs_1_
  60.3 0.0 collective-permute-done.9.refs_3_
  60.3 9.5 %collective-permute-done.8.refs_2_ = bf16[8,16384]{1,0:T(8,128)(2,1)S(1)} collective-permute-done((bf16[8,16384]{1,0:T(8,128)(2,1)S(1)}, bf16[8,16384]{1,0:T(8,128)(2,1)S(1)}, u32[]{:S(2)}, u32[]{:S(2)}) %collective-permute-start.8) | collective-permute-done | bytes 262176 | tf_op jit(solution)/shard_map/ppermute | solution.py:57
  69.8 1.0 collective-permute-done.10.refs_4_
  70.8 0.0 copy-done.1
  70.8 0.7 shard_map.46
  71.5 28.0 %all_to_all.10 = bf16[64,8,512]{2,1,0:T(8,128)(2,1)S(1)} all-to-all(bf16[64,8,512]{2,1,0:T(8,128)(2,1)S(1)} %shard_map.46), channel_id=1, replica_groups=mesh['shard'=64,'rep'=12] {'shard'}, dimensions={0} | all-to-all | bytes 1048576 | tf_op jit(solution)/shard_map/all_to_all | solution.py:255
  99.5 0.0 copy-done
  99.5 0.0 copy-done.2
  99.5 0.6 shard_map.47
  100.1 26.0 %all_to_all.11.returned_ref = bf16[64,8,512]{2,1,0:T(8,128)(2,1)S(1)} all-to-all(bf16[64,8,512]{2,1,0:T(8,128)(2,1)S(1)} %bitcast.14), channel_id=1, replica_groups=mesh['shard'=64,'rep'=12] {'shard'}, dimensions={0} | all-to-all | bytes 1048576 | tf_op jit(solution)/shard_map/all_to_all | solution.py:269
  126.2 1.3 shard_map.48
  (3 shorter events, 0.1 us)
Async XLA Ops:
  1.2 27.4 %collective-permute-start = (bf16[8,16384]{1,0:T(8,128)(2,1)S(1)}, bf16[8,16384]{1,0:T(8,128)(2,1)S(1)}, u32[]{:S(2)}, u32[]{:S(2)}) collective-permute-start(bf16[8,16384]{1,0:T(8,128)(2,1)S(1)} %get-tuple-element.29), channel_id=1, source_target_pairs={{0,10},{1,11},{2,0},{3,1},{4,2},{5,3},{6,4},{7,5},{8,6},{9,7},{10,... | collective-permute-start | bytes 786440 | tf_op jit(solution)/shard_map/ppermute | solution.py:57
  7.8 20.8 %collective-permute-start.1 = (bf16[8,16384]{1,0:T(8,128)(2,1)S(1)}, bf16[8,16384]{1,0:T(8,128)(2,1)S(1)}, u32[]{:S(2)}, u32[]{:S(2)}) collective-permute-start(bf16[8,16384]{1,0:T(8,128)(2,1)S(1)} %get-tuple-element.30), channel_id=1, source_target_pairs={{0,11},{1,0},{2,1},{3,2},{4,3},{5,4},{6,5},{7,6},{8,7},{9,8},{10,9... | collective-permute-start | bytes 786440 | tf_op jit(solution)/shard_map/ppermute | solution.py:57
  11.8 16.7 %collective-permute-start.2 = (bf16[8,16384]{1,0:T(8,128)(2,1)S(1)}, bf16[8,16384]{1,0:T(8,128)(2,1)S(1)}, u32[]{:S(2)}, u32[]{:S(2)}) collective-permute-start(bf16[8,16384]{1,0:T(8,128)(2,1)S(1)} %get-tuple-element.32), channel_id=1, source_target_pairs={{0,1},{1,2},{2,3},{3,4},{4,5},{5,6},{6,7},{7,8},{8,9},{9,10},{10,1... | collective-permute-start | bytes 786440 | tf_op jit(solution)/shard_map/ppermute | solution.py:57
  22.1 48.7 %copy-start.1 = (s32[1,32]{1,0:T(1,128)S(1)}, s32[1,32]{1,0:T(1,128)}, u32[]{:S(2)}) copy-start(s32[1,32]{1,0:T(1,128)} %param.5) | copy-start | bytes 388
  22.1 20.1 %collective-permute-start.4 = (bf16[8,16384]{1,0:T(8,128)(2,1)S(1)}, bf16[8,16384]{1,0:T(8,128)(2,1)S(1)}, u32[]{:S(2)}, u32[]{:S(2)}) collective-permute-start(bf16[8,16384]{1,0:T(8,128)(2,1)S(1)} %get-tuple-element.39), channel_id=1, source_target_pairs={{0,11},{1,0},{2,1},{3,2},{4,3},{5,4},{6,5},{7,6},{8,7},{9,8},{10,9... | collective-permute-start | bytes 786440 | tf_op jit(solution)/shard_map/ppermute | solution.py:57
  28.6 70.9 %copy-start = (bf16[1,1,2,512,512]{4,3,2,1,0:T(8,128)(2,1)S(1)}, bf16[1,1,2,512,512]{4,3,2,1,0:T(8,128)(2,1)}, u32[]{:S(2)}) copy-start(bf16[1,1,2,512,512]{4,3,2,1,0:T(8,128)(2,1)} %param.7) | copy-start | bytes 3145732
  28.6 70.9 %copy-start.2 = (s32[1,16]{1,0:T(1,128)S(1)}, s32[1,16]{1,0:T(1,128)}, u32[]{:S(2)}) copy-start(s32[1,16]{1,0:T(1,128)} %param.6) | copy-start | bytes 196
  28.6 17.0 %collective-permute-start.5 = (bf16[8,16384]{1,0:T(8,128)(2,1)S(1)}, bf16[8,16384]{1,0:T(8,128)(2,1)S(1)}, u32[]{:S(2)}, u32[]{:S(2)}) collective-permute-start(bf16[8,16384]{1,0:T(8,128)(2,1)S(1)} %add_add_fusion.2), channel_id=1, source_target_pairs={{0,10},{1,11},{2,0},{3,1},{4,2},{5,3},{6,4},{7,5},{8,6},{9,7},{10,... | collective-permute-start | bytes 786440 | tf_op jit(solution)/shard_map/ppermute | solution.py:57
  30.7 15.0 %collective-permute-start.6 = (bf16[8,16384]{1,0:T(8,128)(2,1)S(1)}, bf16[8,16384]{1,0:T(8,128)(2,1)S(1)}, u32[]{:S(2)}, u32[]{:S(2)}) collective-permute-start(bf16[8,16384]{1,0:T(8,128)(2,1)S(1)} %get-tuple-element.42), channel_id=1, source_target_pairs={{0,1},{1,2},{2,3},{3,4},{4,5},{5,6},{6,7},{7,8},{8,9},{9,10},{10,1... | collective-permute-start | bytes 786440 | tf_op jit(solution)/shard_map/ppermute | solution.py:57
  36.0 24.2 %collective-permute-start.3 = (bf16[8,16384]{1,0:T(8,128)(2,1)S(1)}, bf16[8,16384]{1,0:T(8,128)(2,1)S(1)}, u32[]{:S(2)}, u32[]{:S(2)}) collective-permute-start(bf16[8,16384]{1,0:T(8,128)(2,1)S(1)} %get-tuple-element.35), channel_id=1, source_target_pairs={{0,11},{1,0},{2,1},{3,2},{4,3},{5,4},{6,5},{7,6},{8,7},{9,8},{10,9... | collective-permute-start | bytes 786440 | tf_op jit(solution)/shard_map/ppermute | solution.py:57
  38.0 14.3 %collective-permute-start.7 = (bf16[8,16384]{1,0:T(8,128)(2,1)S(1)}, bf16[8,16384]{1,0:T(8,128)(2,1)S(1)}, u32[]{:S(2)}, u32[]{:S(2)}) collective-permute-start(bf16[8,16384]{1,0:T(8,128)(2,1)S(1)} %add.216), channel_id=1, source_target_pairs={{0,2},{1,3},{2,4},{3,5},{4,6},{5,7},{6,8},{7,9},{8,10},{9,11},{10,... | collective-permute-start | bytes 786440 | tf_op jit(solution)/shard_map/ppermute | solution.py:57
  42.2 18.0 %collective-permute-start.9 = (bf16[8,16384]{1,0:T(8,128)(2,1)S(1)}, bf16[8,16384]{1,0:T(8,128)(2,1)S(1)}, u32[]{:S(2)}, u32[]{:S(2)}) collective-permute-start(bf16[8,16384]{1,0:T(8,128)(2,1)S(1)} %get-tuple-element.45), channel_id=1, source_target_pairs={{0,1},{1,2},{2,3},{3,4},{4,5},{5,6},{6,7},{7,8},{8,9},{9,10},{10,1... | collective-permute-start | bytes 786440 | tf_op jit(solution)/shard_map/ppermute | solution.py:57
  52.3 17.5 %collective-permute-start.8 = (bf16[8,16384]{1,0:T(8,128)(2,1)S(1)}, bf16[8,16384]{1,0:T(8,128)(2,1)S(1)}, u32[]{:S(2)}, u32[]{:S(2)}) collective-permute-start(bf16[8,16384]{1,0:T(8,128)(2,1)S(1)} %add_add_fusion.1), channel_id=1, source_target_pairs={{0,10},{1,11},{2,0},{3,1},{4,2},{5,3},{6,4},{7,5},{8,6},{9,7},{10,... | collective-permute-start | bytes 786440 | tf_op jit(solution)/shard_map/ppermute | solution.py:57
  57.4 13.5 %collective-permute-start.10 = (bf16[8,16384]{1,0:T(8,128)(2,1)S(1)}, bf16[8,16384]{1,0:T(8,128)(2,1)S(1)}, u32[]{:S(2)}, u32[]{:S(2)}) collective-permute-start(bf16[8,16384]{1,0:T(8,128)(2,1)S(1)} %add_add_fusion), channel_id=1, source_target_pairs={{0,2},{1,3},{2,4},{3,5},{4,6},{5,7},{6,8},{7,9},{8,10},{9,11},{10,... | collective-permute-start | bytes 786440 | tf_op jit(solution)/shard_map/ppermute | solution.py:57
